TPU v7x, 128 devices: a whole 4x4x4 slice. The times are simulated.
128 devices in a mesh: data: 64 (over z, y, x), model: 2 (over core).
Axes of the slice: x: 4, y: 4, z: 4, core: 2. Of those that a mesh axis runs over, the one named last changes fastest.
Arguments:
- teacher_in: bfloat16 [512, 512, 1024], P('data', 'model')
- student_in: bfloat16 [512, 512, 384], P(('data', 'model'))
- teacher_gain: float32 [2, 1024], replicated
- teacher_up: bfloat16 [2, 1024, 4096], P(None, None, 'model')
- teacher_down: bfloat16 [2, 4096, 1024], P(None, 'model')
- student_gain: float32 [1, 384], replicated
- student_up: bfloat16 [1, 384, 1536], replicated
- student_down: bfloat16 [1, 1536, 384], replicated
- student_proj: bfloat16 [1, 1024, 384], replicated
Outputs:
- output 1: float32 [], replicated
- output 2: float32 [1, 384, 1536], replicated
- output 3: float32 [1, 1536, 384], replicated
- output 4: float32 [1, 384], replicated
- output 5: float32 [1, 1024, 384], replicated
All inputs are finite; a program needn't handle non-finite values.
Results may differ from a plain program's by a relative error of at most 0.00142751.
Values are sent between devices in bfloat16 or wider.
A program may use at most 1 GiB of HBM per device.

v0:
```python
import functools

import jax
import jax.numpy as jnp
from jax import lax
from jax.experimental import pallas as pl
from jax.experimental.pallas import tpu as pltpu
from jax.sharding import PartitionSpec as P

EPS = 1e-6
F32 = jnp.float32
BF16 = jnp.bfloat16
MESH = pl.DeviceIdType.MESH
ROWS = 512
VMEM_MAX = 62 * 2**20
GELU_A = 0.7978845608028654
GELU_B = 0.044715


def rms_unit(values):
    return values * lax.rsqrt(jnp.mean(values * values, axis=-1, keepdims=True) + EPS)


def rms_back(values, grad_out):
    inv_rms = lax.rsqrt(jnp.mean(values * values, axis=-1, keepdims=True) + EPS)
    unit = values * inv_rms
    return inv_rms * (grad_out - unit * jnp.mean(grad_out * unit, axis=-1, keepdims=True))


def gelu(pre):
    half = 0.5 * pre
    return half + half * jnp.tanh(pre * (GELU_A + (GELU_A * GELU_B) * (pre * pre)))


def rows_of(blk):
    return pl.ds(pl.multiple_of(blk * ROWS, ROWS), ROWS)


def partner():
    return {"model": 1 - lax.axis_index("model")}


def greet_partner():
    barrier = pltpu.get_barrier_semaphore()
    pl.semaphore_signal(barrier, inc=1, device_id=partner(), device_id_type=MESH)
    pl.semaphore_wait(barrier, 1)


def teacher_kernel(n_blk, h_in, gain, up, down, stud, f_out, stud_r, h_v, a_v, acc_v, p_v, up_v, down_v, h_sem, w_sem, o_sem, send_sem, recv_sem):
    half = up_v.shape[2] // 2
    n_tok = h_v.shape[0]

    def blk(b):
        return pl.ds(pl.multiple_of(b * ROWS, ROWS), ROWS)

    h_loads = [pltpu.make_async_copy(h_in.at[blk(b)], h_v.at[blk(b)], h_sem.at[b]) for b in range(n_blk)]
    w_loads = [
        [
            pltpu.make_async_copy(up.at[layer, :, pl.ds(part * half, half)], up_v.at[2 * layer, :, pl.ds(part * half, half)], w_sem.at[layer, part])
            for part in range(2)
        ]
        + [pltpu.make_async_copy(down.at[layer], down_v.at[2 * layer], w_sem.at[layer, 2])]
        for layer in range(2)
    ]
    for load in h_loads + w_loads[0]:
        load.start()
    greet_partner()
    swaps = []
    for layer in range(2):
        group = []
        for idx, (src, dst) in enumerate([(up, up_v), (down, down_v)]):
            step = src.shape[1] // 4
            for piece in range(4):
                rows = pl.ds(piece * step, step)
                sems = (layer, idx, piece)
                group.append(pltpu.make_async_remote_copy(
                    src_ref=src.at[layer, rows], dst_ref=dst.at[2 * layer + 1, rows],
                    send_sem=send_sem.at[sems], recv_sem=recv_sem.at[sems], device_id=partner(), device_id_type=MESH))
        swaps.append(group)
    for copy in swaps[0]:
        copy.start()
    for load in w_loads[1]:
        load.start()
    half_len = stud.shape[1] // 2
    give = pl.ds(pl.multiple_of((1 - lax.axis_index("model")) * half_len, half_len), half_len)
    last = (2, 0, 0)
    swaps[1].append(pltpu.make_async_remote_copy(src_ref=stud.at[:, give], dst_ref=stud_r, send_sem=send_sem.at[last], recv_sem=recv_sem.at[last], device_id=partner(), device_id_type=MESH))
    for copy in swaps[1]:
        copy.start()

    def norm(b, layer):
        a_v[blk(b), :] = (rms_unit(h_v[blk(b), :].astype(F32)) * gain[pl.ds(layer, 1), :]).astype(BF16)

    def up_part(unit, part):
        cols = pl.ds(part * half, half)
        p_v[part] = jnp.dot(a_v[blk(unit % n_blk), :], up_v[unit // n_blk, :, cols], preferred_element_type=F32)

    def down_part(unit, part):
        acc_v[blk(unit % n_blk), :] += jnp.dot(gelu(p_v[part]).astype(BF16), down_v[unit // n_blk, pl.ds(part * half, half), :], preferred_element_type=F32)

    def finish(b, layer):
        h_v[blk(b), :] = (h_v[blk(b), :].astype(F32) + acc_v[blk(b), :].astype(BF16).astype(F32)).astype(BF16)
        acc_v[blk(b), :] = jnp.zeros((ROWS, acc_v.shape[1]), F32)
        norm(b, jnp.minimum(layer + 1, 1))

    def out(b):
        return pltpu.make_async_copy(h_v.at[blk(b)], f_out.at[blk(b)], o_sem.at[b])

    def clear(i, carry):
        acc_v[pl.ds(pl.multiple_of(i * 64, 64), 64), :] = jnp.zeros((64, acc_v.shape[1]), F32)
        return carry

    lax.fori_loop(0, n_tok // 64, clear, 0)
    h_loads[0].wait()
    norm(0, 0)
    w_loads[0][0].wait()
    up_part(0, 0)
    for load in h_loads[1:]:
        load.wait()

    def norm_step(b, carry):
        norm(b, 0)
        return carry

    lax.fori_loop(1, n_blk, norm_step, 0)
    for load in w_loads[0][1:]:
        load.wait()
    end = 4 * n_blk

    def arrive(unit, at, copies, remote):
        @pl.when(unit == at)
        def _():
            for copy in copies:
                if remote:
                    copy.wait_recv()
                else:
                    copy.wait()

    def layer_step(layer, carry):
        def plain(unit, inner):
            arrive(unit, n_blk - 1, swaps[0], True)
            arrive(unit, 3 * n_blk - 1, swaps[1], True)
            up_part(unit, 1)
            down_part(unit, 0)
            up_part(unit + 1, 0)
            down_part(unit, 1)
            return inner

        def closing(unit, inner):
            arrive(unit, 2 * n_blk - 1, w_loads[1], False)
            done = unit - (n_blk + 1) - 2 * n_blk * layer
            up_part(unit, 1)
            down_part(unit, 0)
            finish(done, layer)
            up_part(jnp.minimum(unit + 1, end - 1), 0)
            down_part(unit, 1)

            @pl.when(layer == 1)
            def _():
                out(done).start()

            return inner

        lax.fori_loop((2 * n_blk + 1) * layer, (n_blk + 1) + 2 * n_blk * layer, plain, 0)
        lax.fori_loop((n_blk + 1) + 2 * n_blk * layer, (2 * n_blk + 1) + (2 * n_blk - 1) * layer, closing, 0)
        return carry

    lax.fori_loop(0, 2, layer_step, 0)
    b_last = n_blk - 1
    h_v[blk(b_last), :] = (h_v[blk(b_last), :].astype(F32) + acc_v[blk(b_last), :].astype(BF16).astype(F32)).astype(BF16)
    out(b_last).start()
    for b in range(n_blk):
        out(b).wait()
    for group in swaps:
        for copy in group:
            copy.wait_send()


def any_specs(count):
    return [pl.BlockSpec(memory_space=pl.ANY)] * count


VM = pl.BlockSpec(memory_space=pltpu.VMEM)


def teacher(tokens, gain, up, down, stud):
    n_tok, width = tokens.shape
    cols = up.shape[2]
    n_blk = n_tok // ROWS
    seqs, length, s_width = stud.shape
    dma, vmem = pltpu.SemaphoreType.DMA, pltpu.VMEM
    v_tok = vmem((n_tok, width), BF16)
    return pl.pallas_call(
        functools.partial(teacher_kernel, n_blk),
        out_shape=(jax.ShapeDtypeStruct((n_tok, width), BF16), jax.ShapeDtypeStruct((seqs, length // 2, s_width), BF16)),
        in_specs=[pl.BlockSpec(memory_space=pl.ANY), VM] + any_specs(3),
        out_specs=any_specs(2),
        scratch_shapes=[v_tok, v_tok, vmem((n_tok, width), F32), vmem((2, ROWS, cols // 2), F32), vmem((4, width, cols), BF16), vmem((4, cols, width), BF16),
                        dma((n_blk,)), dma((2, 3)), dma((n_blk,)), dma((3, 2, 4)), dma((3, 2, 4))],
        compiler_params=pltpu.CompilerParams(collective_id=0, has_side_effects=True, vmem_limit_bytes=VMEM_MAX),
        cost_estimate=pl.CostEstimate(flops=16 * n_tok * width * cols, bytes_accessed=2**25, transcendentals=0),
        name="teacher",
    )(tokens, gain, up, down, stud)


PART = 128
SIDE = PART // 2
RING = 4
STRIDES = (1, RING, RING * RING)
OTHERS = (2, 1, 3)


def gelu_pair(pre):
    sq = pre * pre
    tanh = jnp.tanh(pre * (GELU_A + (GELU_A * GELU_B) * sq))
    cdf = 0.5 + 0.5 * tanh
    slope = cdf + (0.5 * pre) * ((1.0 - tanh * tanh) * (GELU_A + (3.0 * GELU_A * GELU_B) * sq))
    return pre * cdf, slope


def dot_rows(lhs, rhs):
    return lax.dot_general(lhs, rhs, (((0,), (0,)), ((), ())), preferred_element_type=F32)


def dot_cols(lhs, rhs):
    return lax.dot_general(lhs, rhs, (((1,), (1,)), ((), ())), preferred_element_type=F32)


def axis_coord(stride):
    return (lax.axis_index("data") // stride) % RING


def axis_peer(stride, offset):
    coord = axis_coord(stride)
    return {"data": lax.axis_index("data") + (((coord + offset) % RING) - coord) * stride}


def span(index, size):
    return pl.ds(pl.multiple_of(index * size, size), size)


class PartSum:
    def __init__(self, ops, credit, g_v, bufs, part, first_col, n_cols):
        self.sender, self.credit, self.g_v, self.part = ops, credit, g_v, part
        self.core_v, self.fwd_v, self.fsum_v, self.near_v, self.p2_v, self.r2_v, self.slots_v = [buf.at[part] for buf in bufs]
        self.wide = n_cols // RING
        self.first_col, self.n_cols = first_col, n_cols
        self.axes = [STRIDES[(part + i) % len(STRIDES)] for i in range(len(STRIDES))]
        self.coords = [axis_coord(stride) for stride in self.axes]
        self.row0 = part * PART + lax.axis_index("model") * SIDE
        self.up, self.down = axis_peer(self.axes[0], 1), axis_peer(self.axes[0], RING - 1)
        self.cols = pl.ds(first_col, n_cols)

    def rows(self, offset, size):
        return pl.ds(pl.multiple_of(self.row0 + offset, size), size)

    def lanes(self, shift):
        return span((self.coords[0] + shift) % RING, self.wide)

    def out(self, offset, size, shift):
        lanes = pl.ds(pl.multiple_of(self.first_col + ((self.coords[0] + shift) % RING) * self.wide, 128), self.wide)
        return self.g_v.at[self.rows(offset, size), lanes]

    def core_send(self):
        away = pl.ds(pl.multiple_of(self.part * PART + (1 - lax.axis_index("model")) * SIDE, SIDE), SIDE)
        self.core = self.sender(self.g_v.at[away, self.cols], self.core_v, partner(), True)

    def ring_start(self):
        self.core.wait()
        pl.semaphore_signal(self.credit, inc=1, device_id=partner(), device_id_type=MESH)
        self.core_v[...] = self.core_v[...] + self.g_v[self.rows(0, SIDE), self.cols]
        half = SIDE // 2
        lo, hi = pl.ds(0, half), pl.ds(half, half)
        self.fwd = [self.sender(self.core_v.at[lo, self.lanes(2)], self.fwd_v.at[0], self.up), self.sender(self.core_v.at[hi, self.lanes(2)], self.fwd_v.at[1], self.down)]
        self.near = [self.sender(self.core_v.at[hi, self.lanes(1)], self.near_v.at[0, hi], self.up), self.sender(self.core_v.at[lo, self.lanes(3)], self.near_v.at[1, lo], self.down)]

    def ring_forward(self):
        half = SIDE // 2
        for which, shift, dev in ((0, 1, self.up), (1, 3, self.down)):
            rows = pl.ds(which * half, half)
            self.fwd[which].wait_recv()
            self.fsum_v[which] = self.fwd_v[which] + self.core_v[rows, self.lanes(shift)]
            self.near.append(self.sender(self.fsum_v.at[which], self.near_v.at[which, rows], dev))

    def second_start(self):
        for copy in self.near:
            copy.wait_recv()
        self.p2_v[...] = self.core_v[:, self.lanes(0)] + (self.near_v[0] + self.near_v[1])
        size = SIDE // RING
        self.r2 = [self.sender(self.p2_v.at[span((self.coords[1] + off) % RING, size)], self.r2_v.at[off - 1], axis_peer(self.axes[1], off)) for off in OTHERS]

    def third_start(self):
        for copy in self.r2:
            copy.wait_recv()
        slot = self.slots_v.at[self.coords[2]]
        slot[...] = (self.p2_v[span(self.coords[1], SIDE // RING), :] + self.r2_v[1]) + (self.r2_v[0] + self.r2_v[2])
        self.r3 = [self.sender(slot, slot, axis_peer(self.axes[2], off)) for off in OTHERS]

    def back_second(self):
        for copy in self.r3:
            copy.wait_recv()
        size = SIDE // RING
        block = self.out(self.coords[1] * size, size, 0)
        block[...] = (self.slots_v[0] + self.slots_v[1]) + (self.slots_v[2] + self.slots_v[3])
        self.b2 = [self.sender(block, block, axis_peer(self.axes[1], off)) for off in OTHERS]

    def back_first(self):
        for copy in self.b2:
            copy.wait_recv()
        half = SIDE // 2
        lo, hi = self.out(0, half, 0), self.out(half, half, 0)
        self.early = [self.sender(lo, lo, self.up), self.sender(hi, hi, self.down)]
        self.late = [self.sender(hi, hi, self.up), self.sender(lo, lo, self.down)]
        self.cross = []
        pl.semaphore_wait(self.credit, 1)
        self.give(0)

    def give(self, shift):
        block = self.out(0, SIDE, shift)
        self.cross.append(self.sender(block, block, partner()))

    def back_forward(self):
        half = SIDE // 2
        self.far = []
        for which, shift, dev in ((0, 3, self.up), (1, 1, self.down)):
            self.early[which].wait_recv()
            block = self.out(which * half, half, shift)
            self.far.append(self.sender(block, block, dev))

    def back_core(self):
        for which, shift in ((0, 3), (1, 1)):
            self.late[which].wait_recv()
            self.give(shift)

    def back_last(self):
        for copy in self.far:
            copy.wait_recv()
        self.give(2)

    def finish(self):
        for copy in self.cross:
            copy.wait_recv()


STAGES = ("core_send", "ring_start", "ring_forward", "second_start", "third_start", "back_second", "back_first", "back_forward", "back_core", "back_last", "finish")


class SmallSum:
    def __init__(self, sender, small_v, slots_v):
        self.sender, self.small_v, self.slots_v, self.level = sender, small_v, slots_v, 0

    def send(self):
        level = self.level
        coord = lax.axis_index("model") if level == 0 else axis_coord(STRIDES[level - 1])
        slots = self.slots_v.at[level]
        slots[coord] = self.small_v[level]
        peers = [partner()] if level == 0 else [axis_peer(STRIDES[level - 1], off) for off in OTHERS]
        self.copies = [self.sender(self.small_v.at[level], slots.at[coord], dev) for dev in peers]

    def add(self):
        for copy in self.copies:
            copy.wait_recv()
        slots = self.slots_v.at[self.level]
        total = slots[0] + slots[1]
        if self.level > 0:
            total = total + (slots[2] + slots[3])
        self.level += 1
        self.small_v[self.level] = total


def student_kernel(n_blk, grad_scale, f_in, stud, stud_r, s_gain, s_up, s_down, s_proj, up_out, down_out, proj_out, small_out, f_v, s_v, su_v, sd_v, sp_v, u_v, slope_v, act_v, d_v, e_v, g_v, small_v, slots_v, *rest):
    bufs_a, bufs_b = rest[:7], rest[7:14]
    f_sem, s_sem, o_sem, send_sem, recv_sem, credit = rest[14:]
    core = lax.axis_index("model")
    seqs, half_len, s_width = stud_r.shape
    f_width = s_up.shape[2]
    t_width = s_proj.shape[1]
    keep = span(core, half_len)
    f_loads = [pltpu.make_async_copy(f_in.at[rows_of(b)], f_v.at[rows_of(b)], f_sem.at[b]) for b in range(n_blk)]
    pairs = [(stud.at[:, keep], s_v.at[pl.ds(core * seqs, seqs)]), (stud_r, s_v.at[pl.ds((1 - core) * seqs, seqs)]), (s_up.at[0], su_v), (s_proj.at[0], sp_v), (s_down.at[0], sd_v)]
    s_loads = [pltpu.make_async_copy(src, dst, s_sem.at[i]) for i, (src, dst) in enumerate(pairs)]
    for load in s_loads + f_loads:
        load.start()
    barrier = pltpu.get_barrier_semaphore()
    peers = [partner()] + [axis_peer(stride, off) for stride in STRIDES for off in OTHERS]
    for peer in peers:
        pl.semaphore_signal(barrier, inc=1, device_id=peer, device_id_type=MESH)
    pl.semaphore_wait(barrier, len(peers))
    started = []

    def sender(src, dst, dev, waited=False):
        slot = len(started)
        copy = pltpu.make_async_remote_copy(src_ref=src, dst_ref=dst, send_sem=send_sem.at[slot], recv_sem=recv_sem.at[slot], device_id=dev, device_id_type=MESH)
        copy.start()
        started.append(None if waited else copy)
        return copy

    parts = range(s_width // PART)
    group_a = [PartSum(sender, credit.at[0, k], g_v, bufs_a, k, f_width, f_width + t_width) for k in parts]
    group_b = [PartSum(sender, credit.at[1, k], g_v, bufs_b, k, 0, f_width) for k in parts]
    small = SmallSum(sender, small_v, slots_v)

    def run(group, num):
        for part in group:
            getattr(part, STAGES[num])()

    small_v[0] = jnp.zeros(small_v.shape[1:], F32)
    for load in s_loads + f_loads:
        load.wait()

    def state_of(b):
        n_seq = ROWS // half_len
        return s_v[pl.ds(b * n_seq, n_seq)].reshape(ROWS, s_width).astype(F32)

    def forward(b, carry):
        state = state_of(b)
        target = jnp.dot(f_v[rows_of(b), :], sp_v[...], preferred_element_type=F32).astype(BF16)
        act = (rms_unit(state) * s_gain[...]).astype(BF16)
        act_v[rows_of(b), :] = act
        up_act, slope = gelu_pair(jnp.dot(act, su_v[...], preferred_element_type=F32))
        up_act = up_act.astype(BF16)
        slope_v[rows_of(b), :] = slope
        u_v[rows_of(b), :] = up_act
        new_state = (state + jnp.dot(up_act, sd_v[...], preferred_element_type=F32)).astype(BF16).astype(F32)
        error = target.astype(F32) - rms_unit(new_state)
        small_v[0, 1:2, 0:s_width] += jnp.sum(error * error, axis=0, keepdims=True)
        e_v[rows_of(b), :] = error.astype(BF16)
        d_v[rows_of(b), :] = rms_back(new_state, -grad_scale * error).astype(BF16)
        return carry

    def backward(b, carry):
        u_v[rows_of(b), :] = (slope_v[rows_of(b), :] * dot_cols(d_v[rows_of(b), :], sd_v[...])).astype(BF16)
        return carry

    def gain_sum(b, carry):
        d_act = dot_cols(u_v[rows_of(b), :], su_v[...])
        small_v[0, 0:1, 0:s_width] += jnp.sum(d_act * rms_unit(state_of(b)), axis=0, keepdims=True)
        return carry

    lax.fori_loop(0, n_blk, forward, 0)
    g_v[:, 2 * f_width : 2 * f_width + t_width] = grad_scale * dot_rows(e_v[...], f_v[...])
    g_v[:, f_width : 2 * f_width] = dot_rows(d_v[...], u_v[...])
    run(group_a, 0)
    lax.fori_loop(0, n_blk, backward, 0)
    run(group_a, 1)
    g_v[:, 0:f_width] = dot_rows(act_v[...], u_v[...])
    run(group_b, 0)
    run(group_a, 2)
    lax.fori_loop(0, n_blk // 2, gain_sum, 0)
    run(group_b, 1)
    lax.fori_loop(n_blk // 2, n_blk, gain_sum, 0)
    small_v[0, 2:3, 0:PART] = jnp.broadcast_to(jnp.sum(small_v[0, 1:2, 0:s_width], axis=1, keepdims=True), (1, PART))
    small.send()
    for num in range(2, len(STAGES)):
        run(group_b, num)
        if num + 1 < len(STAGES):
            run(group_a, num + 1)
        if small.level <= len(STRIDES):
            small.add()
            if small.level <= len(STRIDES):
                small.send()
            else:
                small_out[...] = small_v[small.level]
    outs = [pltpu.make_async_copy(g_v.at[:, pl.ds(col, out.shape[1])], out, o_sem.at[i]) for i, (col, out) in enumerate([(0, up_out), (f_width, down_out), (2 * f_width, proj_out)])]
    for out in outs:
        out.start()
    for out in outs:
        out.wait()
    for copy in started:
        if copy is not None:
            copy.wait_send()


def sum_bufs(parts, n_cols):
    wide, vmem = n_cols // RING, pltpu.VMEM
    half, quarter = SIDE // 2, SIDE // RING
    shapes = [(SIDE, n_cols), (2, half, wide), (2, half, wide), (2, SIDE, wide), (SIDE, wide), (len(OTHERS), quarter, wide), (RING, quarter, wide)]
    return [vmem((parts,) + shape, F32) for shape in shapes]


def student_sums(feat, stud, stud_r, s_gain, s_up, s_down, s_proj, grad_scale):
    n_tok, width = feat.shape
    n_blk = n_tok // ROWS
    seqs, half_len, s_width = stud_r.shape
    f_width = s_up.shape[2]
    n_cols = 2 * f_width + width
    parts = s_width // PART
    dma = pltpu.SemaphoreType.DMA
    vmem = pltpu.VMEM
    v_act = vmem((n_tok, s_width), BF16)
    small = (8, s_width)
    n_copies = 200
    return pl.pallas_call(
        functools.partial(student_kernel, n_blk, grad_scale),
        out_shape=tuple(jax.ShapeDtypeStruct(shape, F32) for shape in ((s_width, f_width), (s_width, f_width), (s_width, width), small)),
        in_specs=any_specs(3) + [VM] + any_specs(3),
        out_specs=any_specs(3) + [VM],
        scratch_shapes=[
            vmem((n_tok, width), BF16), vmem((n_tok // half_len, half_len, s_width), BF16), vmem((s_width, f_width), BF16), vmem((f_width, s_width), BF16), vmem((width, s_width), BF16),
            vmem((n_tok, f_width), BF16), vmem((n_tok, f_width), F32), v_act, v_act, v_act, vmem((s_width, n_cols), F32), vmem((5,) + small, F32), vmem((4, 4) + small, F32)]
        + sum_bufs(parts, f_width + width) + sum_bufs(parts, f_width)
        + [dma((n_blk,)), dma((5,)), dma((3,)), dma((n_copies,)), dma((n_copies,)), pltpu.SemaphoreType.REGULAR((2, parts))],
        compiler_params=pltpu.CompilerParams(collective_id=2, has_side_effects=True, vmem_limit_bytes=VMEM_MAX),
        cost_estimate=pl.CostEstimate(flops=2**34, bytes_accessed=2**24, transcendentals=0),
        name="student_sums",
    )(feat, stud, stud_r, s_gain, s_up, s_down, s_proj)


def solution(mesh):
    dev_count = mesh.shape["data"] * mesh.shape["model"]

    def body(teacher_in, student_in, teacher_gain, teacher_up, teacher_down, student_gain, student_up, student_down, student_proj):
        seq_rows, seq_len, s_width = student_in.shape
        total = seq_rows * dev_count * seq_len * s_width
        grad_scale = 2.0 / total
        t_width = teacher_in.shape[2]
        feat, stud_r = teacher(teacher_in.reshape(-1, t_width), teacher_gain, teacher_up, teacher_down, student_in)
        grad_up, grad_down, grad_proj, small = student_sums(feat, student_in, stud_r, student_gain, student_up, student_down, student_proj, grad_scale)
        return (small[2, 0] / total, grad_up[None], grad_down.T[None], small[0:1, 0:s_width], grad_proj.T[None])

    return jax.shard_map(
        body,
        mesh=mesh,
        in_specs=(
            P("data", "model", None),
            P(("data", "model"), None, None),
            P(),
            P(None, None, "model"),
            P(None, "model", None),
            P(),
            P(),
            P(),
            P(),
        ),
        out_specs=(P(), P(), P(), P(), P()),
        check_vma=False,
    )
```

profile of v0, /device:TPU:1, one launch (start us, length us, event | category | flops | bytes accessed | tf_op | source)
XLA Modules:
  0.0 176.1 jit_solution(3372073629743066676)
XLA Ops:
  0.6 87.1 %teacher.1 = (bf16[2048,1024]{1,0:T(8,128)(2,1)}, bf16[4,256,384]{2,1,0:T(8,128)(2,1)}) custom-call(bf16[2048,1024]{1,0:T(8,128)(2,1)} %bitcast.12, f32[2,1024]{1,0:T(2,128)} %gain.1, bf16[2,1024,2048]{2,1,0:T(8,128)(2,1)} %up.1, bf16[2,2048,1024]{2,1,0:T(8,128)(2,1)} %down.1, bf16[4,512,384]{2,1,0:T(8,128)(2,1)} %stud.3), custom_call_target="tpu_custom_call" | custom-call | flops 68719476736 | bytes 33554432 | tf_op jit(solution)/shard_map/teacher/pallas_call | solution.py:193
  87.8 76.4 %student_sums.1 = (f32[384,1536]{1,0:T(8,128)}, f32[384,1536]{1,0:T(8,128)}, f32[384,1024]{1,0:T(8,128)}, f32[8,384]{1,0:T(8,128)}) custom-call(bf16[2048,1024]{1,0:T(8,128)(2,1)} %get-tuple-element.11.f_in, bf16[4,512,384]{2,1,0:T(8,128)(2,1)} %stud.3, bf16[4,256,384]{2,1,0:T(8,128)(2,1)} %get-tuple-element.12.stud_r, f32[1,384]{1,0:T(1,128)} %s_gain.1, ...), custom_call_target="tpu_custom_call" | custom-call | flops 17179869184 | bytes 16777216 | tf_op jit(solution)/shard_map/student_sums/pallas_call | solution.py:493
  164.2 1.2 slice.6
  166.0 3.0 %copy.14 = f32[1,1536,384]{2,1,0:T(8,128)} copy(f32[1,1536,384]{1,2,0:T(8,128)} %bitcast.10) | data formatting | bytes 4718592
  169.1 0.0 copy-start
  169.1 1.4 slice.7
  170.5 3.0 %copy.15 = f32[1,1024,384]{2,1,0:T(8,128)} copy(f32[1,1024,384]{1,2,0:T(8,128)} %bitcast.11) | data formatting | bytes 3145728
  173.5 0.0 copy-done
  173.5 1.4 copy.17
Async XLA Ops:
  169.1 4.4 %copy-start = (f32[384,1536]{1,0:T(8,128)S(1)}, f32[384,1536]{1,0:T(8,128)}, u32[]{:S(2)}) copy-start(f32[384,1536]{1,0:T(8,128)} %get-tuple-element.14) | copy-start | bytes 7077892
where the time goes:
time: 176 us
  Pallas kernels  164 us (93%)
  local copies, waits for them, and re-layouts  10.1 us (6%)
  between operations  2.43 us (1%)
    pallas_call x1, Pallas kernels, teacher(): pl.pallas_call(functools.partial(teacher_kernel, n_blk), out_shape=(jax.S...  87.1 us
    pallas_call x1, Pallas kernels, student_sums(): pl.pallas_call(functools.partial(student_kernel, n_blk, grad_scale), out_...  76.4 us
    unnamed x5, local copies, waits for them, and re-layouts  7.48 us

commit v1 on v0

--- a/solution.py
+++ b/solution.py
@@ -46,7 +46,7 @@
     pl.semaphore_wait(barrier, 1)
 
 
-def teacher_kernel(n_blk, h_in, gain, up, down, stud, f_out, stud_r, h_v, a_v, acc_v, p_v, up_v, down_v, h_sem, w_sem, o_sem, send_sem, recv_sem):
+def teacher_kernel(n_blk, h_in, gain, up, down, stud, f_out, stud_r, h_v, a_v, next_v, acc_v, p_v, up_v, down_v, h_sem, w_sem, o_sem, send_sem, recv_sem):
     half = up_v.shape[2] // 2
     n_tok = h_v.shape[0]
 
@@ -88,8 +88,11 @@
     for copy in swaps[1]:
         copy.start()
 
+    def normed(b, layer):
+        return (rms_unit(h_v[blk(b), :].astype(F32)) * gain[pl.ds(layer, 1), :]).astype(BF16)
+
     def norm(b, layer):
-        a_v[blk(b), :] = (rms_unit(h_v[blk(b), :].astype(F32)) * gain[pl.ds(layer, 1), :]).astype(BF16)
+        a_v[blk(b), :] = normed(b, layer)
 
     def up_part(unit, part):
         cols = pl.ds(part * half, half)
@@ -101,7 +104,7 @@
     def finish(b, layer):
         h_v[blk(b), :] = (h_v[blk(b), :].astype(F32) + acc_v[blk(b), :].astype(BF16).astype(F32)).astype(BF16)
         acc_v[blk(b), :] = jnp.zeros((ROWS, acc_v.shape[1]), F32)
-        norm(b, jnp.minimum(layer + 1, 1))
+        next_v[...] = normed(b, jnp.minimum(layer + 1, 1))
 
     def out(b):
         return pltpu.make_async_copy(h_v.at[blk(b)], f_out.at[blk(b)], o_sem.at[b])
@@ -149,11 +152,12 @@
         def closing(unit, inner):
             arrive(unit, 2 * n_blk - 1, w_loads[1], False)
             done = unit - (n_blk + 1) - 2 * n_blk * layer
+            finish(done, layer)
             up_part(unit, 1)
             down_part(unit, 0)
-            finish(done, layer)
             up_part(jnp.minimum(unit + 1, end - 1), 0)
             down_part(unit, 1)
+            a_v[blk(done), :] = next_v[...]
 
             @pl.when(layer == 1)
             def _():
@@ -195,7 +199,7 @@
         out_shape=(jax.ShapeDtypeStruct((n_tok, width), BF16), jax.ShapeDtypeStruct((seqs, length // 2, s_width), BF16)),
         in_specs=[pl.BlockSpec(memory_space=pl.ANY), VM] + any_specs(3),
         out_specs=any_specs(2),
-        scratch_shapes=[v_tok, v_tok, vmem((n_tok, width), F32), vmem((2, ROWS, cols // 2), F32), vmem((4, width, cols), BF16), vmem((4, cols, width), BF16),
+        scratch_shapes=[v_tok, v_tok, vmem((ROWS, width), BF16), vmem((n_tok, width), F32), vmem((2, ROWS, cols // 2), F32), vmem((4, width, cols), BF16), vmem((4, cols, width), BF16),
                         dma((n_blk,)), dma((2, 3)), dma((n_blk,)), dma((3, 2, 4)), dma((3, 2, 4))],
         compiler_params=pltpu.CompilerParams(collective_id=0, has_side_effects=True, vmem_limit_bytes=VMEM_MAX),
         cost_estimate=pl.CostEstimate(flops=16 * n_tok * width * cols, bytes_accessed=2**25, transcendentals=0),
@@ -405,7 +409,7 @@
             getattr(part, STAGES[num])()
 
     small_v[0] = jnp.zeros(small_v.shape[1:], F32)
-    for load in s_loads + f_loads:
+    for load in s_loads:
         load.wait()
 
     def state_of(b):
@@ -413,6 +417,7 @@
         return s_v[pl.ds(b * n_seq, n_seq)].reshape(ROWS, s_width).astype(F32)
 
     def forward(b, carry):
+        pltpu.make_async_copy(f_in.at[rows_of(b)], f_v.at[rows_of(b)], f_sem.at[b]).wait()
         state = state_of(b)
         target = jnp.dot(f_v[rows_of(b), :], sp_v[...], preferred_element_type=F32).astype(BF16)
         act = (rms_unit(state) * s_gain[...]).astype(BF16)
@@ -506,6 +511,33 @@
     )(feat, stud, stud_r, s_gain, s_up, s_down, s_proj)
 
 
+def unpack_kernel(inv_total, up_in, down_in, proj_in, small, up_out, down_out, proj_out, gain_out, loss_out):
+    up_out[0] = up_in[...]
+    down_out[0] = down_in[...].T
+    proj_out[0] = proj_in[...].T
+    gain_out[...] = small[0:1, :]
+    loss_out[...] = small[2:3, 0:1] * inv_total
+
+
+def unpack(grads_up, grads_down, grads_proj, small, total):
+    rows, cols = grads_up.shape
+    width = grads_proj.shape[1]
+    steps = rows // PART
+
+    def block(shape, index):
+        return pl.BlockSpec(shape, index)
+
+    return pl.pallas_call(
+        functools.partial(unpack_kernel, 1.0 / total),
+        grid=(steps,),
+        out_shape=tuple(jax.ShapeDtypeStruct(shape, F32) for shape in ((1, rows, cols), (1, cols, rows), (1, width, rows), (1, rows), (1, 1))),
+        in_specs=[block((PART, cols), lambda i: (i, 0)), block((PART, cols), lambda i: (i, 0)), block((PART, width), lambda i: (i, 0)), block(small.shape, lambda i: (0, 0))],
+        out_specs=(block((1, PART, cols), lambda i: (0, i, 0)), block((1, cols, PART), lambda i: (0, 0, i)), block((1, width, PART), lambda i: (0, 0, i)), block((1, rows), lambda i: (0, 0)), block((1, 1), lambda i: (0, 0))),
+        compiler_params=pltpu.CompilerParams(vmem_limit_bytes=VMEM_MAX),
+        name="unpack",
+    )(grads_up, grads_down, grads_proj, small)
+
+
 def solution(mesh):
     dev_count = mesh.shape["data"] * mesh.shape["model"]
 
@@ -516,7 +548,8 @@
         t_width = teacher_in.shape[2]
         feat, stud_r = teacher(teacher_in.reshape(-1, t_width), teacher_gain, teacher_up, teacher_down, student_in)
         grad_up, grad_down, grad_proj, small = student_sums(feat, student_in, stud_r, student_gain, student_up, student_down, student_proj, grad_scale)
-        return (small[2, 0] / total, grad_up[None], grad_down.T[None], small[0:1, 0:s_width], grad_proj.T[None])
+        grad_up, grad_down, grad_proj, grad_gain, loss = unpack(grad_up, grad_down, grad_proj, small, total)
+        return (loss[0, 0], grad_up, grad_down, grad_gain, grad_proj)
 
     return jax.shard_map(
         body,

time: 176 us -> 169 us (0.960)
  local copies, waits for them, and re-layouts: 10.1 us -> 0 us
  Pallas kernels: 164 us -> 168 us
  between operations: 2.43 us -> 0.65 us
    unnamed x5 -> x0, local copies, waits for them, and re-layouts: 7.48 us -> none
    pallas_call x0 -> x1, Pallas kernels: none -> 6.76 us  [unpack(): pl.pallas_call(functools.partial(unpack_kernel, 1.0 / total), grid=(steps...]
    slice x2 -> x0, local copies, waits for them, and re-layouts: 2.61 us -> none  [the longest x1 1.42 us: body(): small[0:1, 0:s_width]]
where the time goes in v1:
time: 169 us
  Pallas kernels  168 us (99%)
    pallas_call x1, Pallas kernels, teacher(): pl.pallas_call(functools.partial(teacher_kernel, n_blk), out_shape=(jax.S...  85.6 us
    pallas_call x1, Pallas kernels, student_sums(): pl.pallas_call(functools.partial(student_kernel, n_blk, grad_scale), out_...  76.1 us
    pallas_call x1, Pallas kernels, unpack(): pl.pallas_call(functools.partial(unpack_kernel, 1.0 / total), grid=(steps...  6.76 us

profile of v1, /device:TPU:1, one launch (start us, length us, event | category | flops | bytes accessed | tf_op | source)
XLA Modules:
  0.0 169.1 jit_solution(1924392372325757838)
XLA Ops:
  0.6 85.6 %teacher.1 = (bf16[2048,1024]{1,0:T(8,128)(2,1)}, bf16[4,256,384]{2,1,0:T(8,128)(2,1)}) custom-call(bf16[2048,1024]{1,0:T(8,128)(2,1)} %bitcast.2, f32[2,1024]{1,0:T(2,128)} %gain.1, bf16[2,1024,2048]{2,1,0:T(8,128)(2,1)} %up.1, bf16[2,2048,1024]{2,1,0:T(8,128)(2,1)} %down.1, bf16[4,512,384]{2,1,0:T(8,128)(2,1)} %stud.3), custom_call_target="tpu_custom_call" | custom-call | flops 68719476736 | bytes 33554432 | tf_op jit(solution)/shard_map/teacher/pallas_call | solution.py:197
  86.3 76.1 %student_sums.1 = (f32[384,1536]{1,0:T(8,128)}, f32[384,1536]{1,0:T(8,128)}, f32[384,1024]{1,0:T(8,128)}, f32[8,384]{1,0:T(8,128)}) custom-call(bf16[2048,1024]{1,0:T(8,128)(2,1)} %get-tuple-element.16.f_in, bf16[4,512,384]{2,1,0:T(8,128)(2,1)} %stud.3, bf16[4,256,384]{2,1,0:T(8,128)(2,1)} %get-tuple-element.17.stud_r, f32[1,384]{1,0:T(1,128)} %s_gain.1, ...), custom_call_target="tpu_custom_call" | custom-call | flops 17179869184 | bytes 16777216 | tf_op jit(solution)/shard_map/student_sums/pallas_call | solution.py:498
  162.3 6.8 %unpack.1 = (f32[1,384,1536]{2,1,0:T(8,128)}, f32[1,1536,384]{2,1,0:T(8,128)}, f32[1,1024,384]{2,1,0:T(8,128)}, f32[1,384]{1,0:T(1,128)}, f32[1,1]{1,0:T(1,128)}) custom-call(f32[384,1536]{1,0:T(8,128)} %get-tuple-element.18.up_in, f32[384,1536]{1,0:T(8,128)} %get-tuple-element.19.down_in, f32[384,1024]{1,0:T(8,128)} %get-tuple-element.20.proj_in, ...), custom_call_target="tpu_custom_call" | custom-call | tf_op jit(solution)/shard_map/unpack/pallas_call | solution.py:530

commit v2 on v1

--- a/solution.py
+++ b/solution.py
@@ -442,11 +442,11 @@
         small_v[0, 0:1, 0:s_width] += jnp.sum(d_act * rms_unit(state_of(b)), axis=0, keepdims=True)
         return carry
 
-    lax.fori_loop(0, n_blk, forward, 0)
+    lax.fori_loop(0, n_blk, forward, 0, unroll=2)
     g_v[:, 2 * f_width : 2 * f_width + t_width] = grad_scale * dot_rows(e_v[...], f_v[...])
     g_v[:, f_width : 2 * f_width] = dot_rows(d_v[...], u_v[...])
     run(group_a, 0)
-    lax.fori_loop(0, n_blk, backward, 0)
+    lax.fori_loop(0, n_blk, backward, 0, unroll=2)
     run(group_a, 1)
     g_v[:, 0:f_width] = dot_rows(act_v[...], u_v[...])
     run(group_b, 0)
@@ -456,21 +456,25 @@
     lax.fori_loop(n_blk // 2, n_blk, gain_sum, 0)
     small_v[0, 2:3, 0:PART] = jnp.broadcast_to(jnp.sum(small_v[0, 1:2, 0:s_width], axis=1, keepdims=True), (1, PART))
     small.send()
+    stores = [pltpu.make_async_copy(g_v.at[:, pl.ds(col, out.shape[1])], out, o_sem.at[i]) for i, (col, out) in enumerate([(0, up_out), (f_width, down_out), (2 * f_width, proj_out)])]
+    final = len(STAGES) - 1
     for num in range(2, len(STAGES)):
         run(group_b, num)
-        if num + 1 < len(STAGES):
+        if num == final:
+            stores[0].start()
+        if num < final:
             run(group_a, num + 1)
+            if num + 1 == final:
+                stores[1].start()
+                stores[2].start()
         if small.level <= len(STRIDES):
             small.add()
             if small.level <= len(STRIDES):
                 small.send()
             else:
                 small_out[...] = small_v[small.level]
-    outs = [pltpu.make_async_copy(g_v.at[:, pl.ds(col, out.shape[1])], out, o_sem.at[i]) for i, (col, out) in enumerate([(0, up_out), (f_width, down_out), (2 * f_width, proj_out)])]
-    for out in outs:
-        out.start()
-    for out in outs:
-        out.wait()
+    for store in stores:
+        store.wait()
     for copy in started:
         if copy is not None:
             copy.wait_send()
@@ -522,7 +526,8 @@
 def unpack(grads_up, grads_down, grads_proj, small, total):
     rows, cols = grads_up.shape
     width = grads_proj.shape[1]
-    steps = rows // PART
+    steps = 2
+    col, wid = cols // steps, width // steps
 
     def block(shape, index):
         return pl.BlockSpec(shape, index)
@@ -531,8 +536,8 @@
         functools.partial(unpack_kernel, 1.0 / total),
         grid=(steps,),
         out_shape=tuple(jax.ShapeDtypeStruct(shape, F32) for shape in ((1, rows, cols), (1, cols, rows), (1, width, rows), (1, rows), (1, 1))),
-        in_specs=[block((PART, cols), lambda i: (i, 0)), block((PART, cols), lambda i: (i, 0)), block((PART, width), lambda i: (i, 0)), block(small.shape, lambda i: (0, 0))],
-        out_specs=(block((1, PART, cols), lambda i: (0, i, 0)), block((1, cols, PART), lambda i: (0, 0, i)), block((1, width, PART), lambda i: (0, 0, i)), block((1, rows), lambda i: (0, 0)), block((1, 1), lambda i: (0, 0))),
+        in_specs=[block((rows, col), lambda i: (0, i)), block((rows, col), lambda i: (0, i)), block((rows, wid), lambda i: (0, i)), block(small.shape, lambda i: (0, 0))],
+        out_specs=(block((1, rows, col), lambda i: (0, 0, i)), block((1, col, rows), lambda i: (0, i, 0)), block((1, wid, rows), lambda i: (0, i, 0)), block((1, rows), lambda i: (0, 0)), block((1, 1), lambda i: (0, 0))),
         compiler_params=pltpu.CompilerParams(vmem_limit_bytes=VMEM_MAX),
         name="unpack",
     )(grads_up, grads_down, grads_proj, small)

time: 169 us -> 167 us (0.988)
  Pallas kernels: 168 us -> 166 us
where the time goes in v2:
time: 167 us
  Pallas kernels  166 us (99%)
    pallas_call x1, Pallas kernels, teacher(): pl.pallas_call(functools.partial(teacher_kernel, n_blk), out_shape=(jax.S...  85.6 us
    pallas_call x1, Pallas kernels, student_sums(): pl.pallas_call(functools.partial(student_kernel, n_blk, grad_scale), out_...  75.1 us
    pallas_call x1, Pallas kernels, unpack(): pl.pallas_call(functools.partial(unpack_kernel, 1.0 / total), grid=(steps...  5.46 us

profile of v2, /device:TPU:1, one launch (start us, length us, event | category | flops | bytes accessed | tf_op | source)
XLA Modules:
  0.0 166.9 jit_solution(2000025381088256989)
XLA Ops:
  0.6 85.6 %teacher.1 = (bf16[2048,1024]{1,0:T(8,128)(2,1)}, bf16[4,256,384]{2,1,0:T(8,128)(2,1)}) custom-call(bf16[2048,1024]{1,0:T(8,128)(2,1)} %bitcast.2, f32[2,1024]{1,0:T(2,128)} %gain.1, bf16[2,1024,2048]{2,1,0:T(8,128)(2,1)} %up.1, bf16[2,2048,1024]{2,1,0:T(8,128)(2,1)} %down.1, bf16[4,512,384]{2,1,0:T(8,128)(2,1)} %stud.3), custom_call_target="tpu_custom_call" | custom-call | flops 68719476736 | bytes 33554432 | tf_op jit(solution)/shard_map/teacher/pallas_call | solution.py:197
  86.3 75.1 %student_sums.1 = (f32[384,1536]{1,0:T(8,128)}, f32[384,1536]{1,0:T(8,128)}, f32[384,1024]{1,0:T(8,128)}, f32[8,384]{1,0:T(8,128)}) custom-call(bf16[2048,1024]{1,0:T(8,128)(2,1)} %get-tuple-element.16.f_in, bf16[4,512,384]{2,1,0:T(8,128)(2,1)} %stud.3, bf16[4,256,384]{2,1,0:T(8,128)(2,1)} %get-tuple-element.17.stud_r, f32[1,384]{1,0:T(1,128)} %s_gain.1, ...), custom_call_target="tpu_custom_call" | custom-call | flops 17179869184 | bytes 16777216 | tf_op jit(solution)/shard_map/student_sums/pallas_call | solution.py:502
  161.4 5.5 %unpack.1 = (f32[1,384,1536]{2,1,0:T(8,128)}, f32[1,1536,384]{2,1,0:T(8,128)}, f32[1,1024,384]{2,1,0:T(8,128)}, f32[1,384]{1,0:T(1,128)}, f32[1,1]{1,0:T(1,128)}) custom-call(f32[384,1536]{1,0:T(8,128)} %get-tuple-element.18.up_in, f32[384,1536]{1,0:T(8,128)} %get-tuple-element.19.down_in, f32[384,1024]{1,0:T(8,128)} %get-tuple-element.20.proj_in, ...), custom_call_target="tpu_custom_call" | custom-call | tf_op jit(solution)/shard_map/unpack/pallas_call | solution.py:535

commit v3 on v2

--- a/solution.py
+++ b/solution.py
@@ -155,7 +155,7 @@
             finish(done, layer)
             up_part(unit, 1)
             down_part(unit, 0)
-            up_part(jnp.minimum(unit + 1, end - 1), 0)
+            up_part(unit + 1, 0)
             down_part(unit, 1)
             a_v[blk(done), :] = next_v[...]
 
@@ -166,13 +166,20 @@
             return inner
 
         lax.fori_loop((2 * n_blk + 1) * layer, (n_blk + 1) + 2 * n_blk * layer, plain, 0)
-        lax.fori_loop((n_blk + 1) + 2 * n_blk * layer, (2 * n_blk + 1) + (2 * n_blk - 1) * layer, closing, 0)
+        lax.fori_loop((n_blk + 1) + 2 * n_blk * layer, (2 * n_blk + 1) + 2 * (n_blk - 1) * layer, closing, 0)
         return carry
 
     lax.fori_loop(0, 2, layer_step, 0)
-    b_last = n_blk - 1
-    h_v[blk(b_last), :] = (h_v[blk(b_last), :].astype(F32) + acc_v[blk(b_last), :].astype(BF16).astype(F32)).astype(BF16)
-    out(b_last).start()
+
+    def close(b):
+        h_v[blk(b), :] = (h_v[blk(b), :].astype(F32) + acc_v[blk(b), :].astype(BF16).astype(F32)).astype(BF16)
+        out(b).start()
+
+    close(n_blk - 2)
+    up_part(end - 1, 1)
+    down_part(end - 1, 0)
+    down_part(end - 1, 1)
+    close(n_blk - 1)
     for b in range(n_blk):
         out(b).wait()
     for group in swaps:

time: 167 us -> 166 us (level)
  no operation moved by 1% of the time
where the time goes in v3:
time: 166 us; the launch traced here: 165 us
  Pallas kernels  165 us (99%)
    pallas_call x1, Pallas kernels, teacher(): pl.pallas_call(functools.partial(teacher_kernel, n_blk), out_shape=(jax.S...  84.3 us
    pallas_call x1, Pallas kernels, student_sums(): pl.pallas_call(functools.partial(student_kernel, n_blk, grad_scale), out_...  75 us
    pallas_call x1, Pallas kernels, unpack(): pl.pallas_call(functools.partial(unpack_kernel, 1.0 / total), grid=(steps...  5.46 us

profile of v3, /device:TPU:1, one launch (start us, length us, event | category | flops | bytes accessed | tf_op | source)
XLA Modules:
  0.0 165.4 jit_solution(9497907863759708556)
XLA Ops:
  0.6 84.3 %teacher.1 = (bf16[2048,1024]{1,0:T(8,128)(2,1)}, bf16[4,256,384]{2,1,0:T(8,128)(2,1)}) custom-call(bf16[2048,1024]{1,0:T(8,128)(2,1)} %bitcast.2, f32[2,1024]{1,0:T(2,128)} %gain.1, bf16[2,1024,2048]{2,1,0:T(8,128)(2,1)} %up.1, bf16[2,2048,1024]{2,1,0:T(8,128)(2,1)} %down.1, bf16[4,512,384]{2,1,0:T(8,128)(2,1)} %stud.3), custom_call_target="tpu_custom_call" | custom-call | flops 68719476736 | bytes 33554432 | tf_op jit(solution)/shard_map/teacher/pallas_call | solution.py:204
  84.9 75.0 %student_sums.1 = (f32[384,1536]{1,0:T(8,128)}, f32[384,1536]{1,0:T(8,128)}, f32[384,1024]{1,0:T(8,128)}, f32[8,384]{1,0:T(8,128)}) custom-call(bf16[2048,1024]{1,0:T(8,128)(2,1)} %get-tuple-element.16.f_in, bf16[4,512,384]{2,1,0:T(8,128)(2,1)} %stud.3, bf16[4,256,384]{2,1,0:T(8,128)(2,1)} %get-tuple-element.17.stud_r, f32[1,384]{1,0:T(1,128)} %s_gain.1, ...), custom_call_target="tpu_custom_call" | custom-call | flops 17179869184 | bytes 16777216 | tf_op jit(solution)/shard_map/student_sums/pallas_call | solution.py:509
  159.9 5.5 %unpack.1 = (f32[1,384,1536]{2,1,0:T(8,128)}, f32[1,1536,384]{2,1,0:T(8,128)}, f32[1,1024,384]{2,1,0:T(8,128)}, f32[1,384]{1,0:T(1,128)}, f32[1,1]{1,0:T(1,128)}) custom-call(f32[384,1536]{1,0:T(8,128)} %get-tuple-element.18.up_in, f32[384,1536]{1,0:T(8,128)} %get-tuple-element.19.down_in, f32[384,1024]{1,0:T(8,128)} %get-tuple-element.20.proj_in, ...), custom_call_target="tpu_custom_call" | custom-call | tf_op jit(solution)/shard_map/unpack/pallas_call | solution.py:542
